TPU v7x, 32 devices: a whole 2x2x4 slice. The times are simulated.
32 devices in a mesh: member: 2 (over core), tile: 16 (over z, y, x).
Axes of the slice: x: 2, y: 2, z: 4, core: 2. Of those that a mesh axis runs over, the one named last changes fastest.
Arguments:
- ensemble: bfloat16 [40, 7, 32, 2048], P('member', None, None, 'tile'), may hold values from -6 to 6
- control: bfloat16 [40, 32, 2048], P('member', None, 'tile'), may hold values from -6 to 6
- vert_loc: bfloat16 [32, 32], replicated, may hold values from -1 to 1
- obs_source: int32 [8192, 1], P('tile'), may hold values from 0 to 15; in each aligned block of 512 rows (0 to 511, 512 to 1023, ...) at most 64 rows name the same one
- obs_column: int32 [8192], P('tile'), may hold values from 0 to 127
- obs_slot: int32 [8192], P('tile'), may hold values from 0 to 5
- obs_frac: float32 [8192], P('tile'), may hold values from 0 to 1
- obs_count: int32 [16], P('tile'), may hold values from 1 to 512, 4096 in all
Outputs:
- obs_increment: float32 [32, 8192], P(None, 'tile')
Inputs may be any that keep to these rules, and one draw needn't show every extreme that they name: `obs_source`: among the 512 observation slots of one owner tile, at most 64 name the same source tile, and some source tile is named exactly 64 times. `obs_count`: the counts sum to 4096 and one of them is 512.
All inputs are finite; a program needn't handle non-finite values. No bound on the sum of `obs_count` on one device may be relied on, other than what follows from the above.
Results may differ from a plain program's by a relative error of at most 0.0003.
Values sent between devices are 32-bit elements; how exact they have to be, the bound alone decides.
A program may use at most 64 MiB of HBM per device.

v0:
```python
import functools

import jax
import jax.numpy as jnp
from jax import lax
from jax.experimental import pallas as pl
from jax.experimental.pallas import tpu as pltpu
from jax.sharding import PartitionSpec as P

MESH = pl.DeviceIdType.MESH
LANES = 128
F32 = jnp.float32
BF16 = jnp.bfloat16


def iota(shape, axis):
    return lax.broadcasted_iota(jnp.int32, shape, axis)


def one_hot(condition):
    return jnp.where(condition, F32(1.0), F32(0.0)).astype(BF16)


def dot(a, b):
    return jnp.dot(a, b, preferred_element_type=F32)


def dot_nt(a, b):
    return lax.dot_general(a, b, (((1,), (1,)), ((), ())), preferred_element_type=F32)


def two_pieces(x):
    high = x.astype(BF16)
    return high, (x - high.astype(F32)).astype(BF16)


def turned(x, shift):
    shift = shift % LANES
    return x if shift == 0 else pltpu.roll(x, shift, 1)


def kernel(
    tiles, groups, cap, packs,
    ens_hbm, ctl_hbm, vloc_hbm, source_hbm, column_hbm, slot_hbm, frac_hbm, count_ref,
    out_ref,
    vloc_ref, source_ref, column_ref, slot_ref, frac_ref, ens, ctl, weighted, part, part_in, req_out, req_in, res_out, res_in, place,
    load_sem, part_send, part_recv, req_send, req_recv, res_send, res_recv,
):
    me = lax.axis_index("tile")
    mine = lax.axis_index("member")
    members, slots, levels, cols = ens.shape
    share = levels // groups
    rows = share // packs
    obs = column_ref.shape[1]
    owners = LANES // cap
    spans = tiles * cap // LANES

    def loaded(index, source, target):
        return pltpu.make_async_copy(source, target, load_sem.at[index])

    loads = [
        loaded(0, source_hbm, source_ref), loaded(1, column_hbm, column_ref),
        loaded(2, slot_hbm, slot_ref), loaded(3, frac_hbm, frac_ref),
        loaded(4, vloc_hbm, vloc_ref), loaded(5, ctl_hbm, ctl), loaded(6, ens_hbm, ens),
    ]
    for load in loads[:4]:
        load.start()

    stride = jnp.where(2 * me < tiles, 1, tiles - 1)
    span_stride = jnp.where(2 * me < tiles, 1, spans - 1)
    home = me // owners

    def peer(step):
        return lax.rem(me + stride * step, tiles)

    def span_at(step):
        return lax.rem(home + span_stride * step, spans)

    def partner(step):
        return lax.rem(mine + step, groups)

    def far_first(count, body):
        if count <= 64:
            for index in range(count - 1, 0, -1):
                body(index)
        else:
            lax.fori_loop(1, count, lambda index, carry: (body(index), carry)[1], 0)

    barrier = pltpu.get_barrier_semaphore()

    def greet(index):
        step, side = index // groups, index % groups
        pl.semaphore_signal(
            barrier, inc=1, device_id={"tile": peer(step), "member": partner(side)},
            device_id_type=MESH,
        )

    far_first(tiles * groups, greet)
    for load in loads[4:]:
        load.start()

    for load in loads[:4]:
        load.wait()
    source = source_ref[...]
    hits = source == iota((tiles, obs), 0)
    hits_f = jnp.where(hits, F32(1.0), F32(0.0))
    before = one_hot(iota((LANES, LANES), 0) < iota((LANES, LANES), 1))
    seen = jnp.zeros((tiles, 1), F32)
    ranks = []
    for block in range(obs // LANES):
        hit = hits_f[:, block * LANES:(block + 1) * LANES]
        ahead = dot(hit.astype(BF16), before) + seen
        ranks.append(jnp.sum(ahead * hit, axis=0, keepdims=True))
        seen = seen + jnp.sum(hit, axis=1, keepdims=True)
    rank = jnp.concatenate(ranks, axis=1).astype(jnp.int32)
    spread = one_hot(rank == lax.rem(iota((LANES, obs), 0), cap))
    frac = frac_ref[...]
    frac_0 = frac.astype(BF16).astype(F32)
    frac_1 = (frac - frac_0).astype(BF16).astype(F32)
    frac_2 = frac - frac_0 - frac_1
    values = [column_ref[...].astype(F32), slot_ref[...].astype(F32), frac_0, frac_1, frac_2]
    packed = dot_nt(
        jnp.concatenate([jnp.where(hits, v, F32(0.0)) for v in values], axis=0).astype(BF16), spread
    )
    packed = [packed[i * tiles:(i + 1) * tiles] for i in range(len(values))]
    request = jnp.where(
        iota((tiles, LANES), 1) < cap,
        packed[0] + cols * packed[1],
        packed[2] + packed[3] + packed[4],
    )
    for tile in range(tiles):
        req_out[tile] = request[tile:tile + 1]

    pl.semaphore_wait(barrier, tiles * groups - 1)

    def request_to(tile, slot_of):
        return pltpu.make_async_remote_copy(
            src_ref=req_out.at[tile], dst_ref=req_in.at[slot_of],
            send_sem=req_send.at[tile], recv_sem=req_recv.at[slot_of],
            device_id={"tile": tile, "member": mine}, device_id_type=MESH,
        )

    far_first(tiles, lambda step: request_to(peer(step), me).start())
    req_in[me] = req_out[me]

    batch = max(d for d in range(1, max(1, LANES // levels) + 1) if members % d == 0)
    wide = batch * levels
    repeat = one_hot(lax.rem(iota((wide, levels), 0), levels) == iota((wide, levels), 1))
    for load in loads[4:6]:
        load.wait()
    tall = dot(repeat, vloc_ref[...]).astype(BF16)
    full = dot_nt(tall, repeat)
    factor = jnp.where(
        iota((wide, wide), 0) // levels == iota((wide, wide), 1) // levels, full, F32(0.0)
    ).astype(BF16)
    for step in range(members // batch):
        weighted[step * wide:(step + 1) * wide] = dot(factor, ctl[step * wide:(step + 1) * wide])

    loads[6].wait()
    for slot in range(slots):
        total = jnp.zeros((levels, cols), F32)
        for k in range(members):
            total = total + ens[k, slot].astype(F32) * weighted[k * levels:(k + 1) * levels]
        for group in range(groups):
            part[group, slot] = total[group * share:(group + 1) * share]

    def give(step):
        return pltpu.make_async_remote_copy(
            src_ref=part.at[partner(step)], dst_ref=part_in.at[step - 1],
            send_sem=part_send.at[step - 1], recv_sem=part_recv.at[step - 1],
            device_id={"tile": me, "member": partner(step)}, device_id_type=MESH,
        )

    for step in range(1, groups):
        give(step).start()

    position = source * cap + rank
    place[...] = one_hot(position == iota((tiles * cap, obs), 0))

    for step in range(1, groups):
        give(step).wait_recv()
    increment = part[mine]
    for step in range(1, groups):
        increment = increment + part_in[step - 1]
    pieces = jnp.concatenate(two_pieces(increment.reshape(slots * share, cols)), axis=1)

    def reply_to(tile, side, slot_of, from_group):
        return pltpu.make_async_remote_copy(
            src_ref=res_out.at[tile], dst_ref=res_in.at[from_group, slot_of],
            send_sem=res_send.at[partner(side), tile], recv_sem=res_recv.at[from_group, slot_of],
            device_id={"tile": tile, "member": partner(side)}, device_id_type=MESH,
        )

    def unless_me(step, tile, body):
        if step == 0:
            pl.when(tile != me)(body)
        else:
            body()

    lane = iota((1, LANES), 1)
    for step in range(spans):
        span = span_at(step)
        code = jnp.zeros((1, LANES), F32)
        frac = jnp.zeros((1, LANES), F32)
        for i in range(owners):
            tile = span * owners + i
            unless_me(step, tile, lambda tile=tile: request_to(tile, tile).wait_recv())
            got = req_in[tile]
            here = lane // cap == i
            code = jnp.where(here, turned(got, i * cap), code)
            frac = jnp.where(here, turned(got, i * cap - cap), frac)
        code = code.astype(jnp.int32)
        wanted = code // cols
        column = code - wanted * cols
        columns = dot(pieces, one_hot(lax.rem(iota((2 * cols, LANES), 0), cols) == column))
        answer = jnp.zeros((share, LANES), F32)
        for slot in range(slots):
            weight = jnp.where(
                wanted == slot, 1.0 - frac, jnp.where(wanted + 1 == slot, frac, F32(0.0))
            )
            answer = answer + weight * columns[slot * share:(slot + 1) * share]
        for i in range(owners):
            tile = span * owners + i
            packet = jnp.zeros((rows, LANES), F32)
            for j in range(packs):
                block = answer[j * rows:(j + 1) * rows]
                packet = jnp.where(lane // cap == j, turned(block, (j - i) * cap), packet)
            res_out[tile] = packet
            if step == 0:
                @pl.when(tile == me)
                def _():
                    res_in[mine, me] = packet
            for side in range(groups):
                if side == 0:
                    unless_me(step, tile, lambda tile=tile: reply_to(tile, 0, me, mine).start())
                else:
                    reply_to(tile, side, me, mine).start()

    for step in range(1, groups):
        give(step).wait_send()

    def wait_reply_send(index):
        reply_to(peer(index // groups), index % groups, me, mine).wait_send()

    far_first(tiles, lambda step: request_to(peer(step), me).wait_send())
    far_first(tiles * groups, wait_reply_send)

    live = iota((levels, obs), 1) < count_ref[0]
    both = jnp.zeros((2 * levels, obs), F32)
    for step in range(spans):
        span = span_at(step)
        bands = [jnp.zeros((rows, LANES), F32)] * (groups * packs)
        for side in range(groups):
            for i in range(owners):
                tile = span * owners + i
                body = lambda tile=tile, side=side: reply_to(tile, side, tile, partner(side)).wait_recv()
                if side == 0:
                    unless_me(step, tile, body)
                else:
                    body()
        for group in range(groups):
            for i in range(owners):
                got = res_in[group, span * owners + i]
                for j in range(packs):
                    at = group * packs + j
                    bands[at] = jnp.where(lane // cap == i, turned(got, (i - j) * cap), bands[at])
        high, low = two_pieces(jnp.concatenate(bands, axis=0))
        first = pl.multiple_of(span * LANES, LANES)
        both = both + dot(jnp.concatenate([high, low], axis=0), place[pl.ds(first, LANES)])
    out_ref[...] = jnp.where(live, both[:levels] + both[levels:], F32(0.0))


def on_device(ensemble, control, vert_loc, obs_source, obs_column, obs_slot, obs_frac, obs_count):
    tiles, groups = lax.axis_size("tile"), lax.axis_size("member")
    members, slots, levels, cols = ensemble.shape
    obs = obs_column.shape[0]
    cap = max(4, 2 * obs // tiles)
    share = levels // groups
    packs = max(1, min(LANES // cap, share // 8))
    rows = share // packs
    vmem = pl.BlockSpec(memory_space=pltpu.VMEM)
    hbm = pl.BlockSpec(memory_space=pl.ANY)
    dma = pltpu.SemaphoreType.DMA
    return pl.pallas_call(
        functools.partial(kernel, tiles, groups, cap, packs),
        out_shape=pltpu.VMEM((levels, obs), F32),
        in_specs=[hbm] * 7 + [pl.BlockSpec(memory_space=pltpu.SMEM)],
        out_specs=vmem,
        scratch_shapes=[
            pltpu.VMEM((levels, levels), BF16),
            pltpu.VMEM((1, obs), jnp.int32),
            pltpu.VMEM((1, obs), jnp.int32),
            pltpu.VMEM((1, obs), jnp.int32),
            pltpu.VMEM((1, obs), F32),
            pltpu.VMEM((members, slots, levels, cols), BF16),
            pltpu.VMEM((members * levels, cols), BF16),
            pltpu.VMEM((members * levels, cols), F32),
            pltpu.VMEM((groups, slots, share, cols), F32),
            pltpu.VMEM((max(1, groups - 1), slots, share, cols), F32),
            pltpu.VMEM((tiles, 1, LANES), F32),
            pltpu.VMEM((tiles, 1, LANES), F32),
            pltpu.VMEM((tiles, rows, LANES), F32),
            pltpu.VMEM((groups, tiles, rows, LANES), F32),
            pltpu.VMEM((tiles * cap, obs), BF16),
            dma((7,)),
            dma((max(1, groups - 1),)),
            dma((max(1, groups - 1),)),
            dma((tiles,)),
            dma((tiles,)),
            dma((groups, tiles)),
            dma((groups, tiles)),
        ],
        compiler_params=pltpu.CompilerParams(collective_id=0, has_side_effects=True),
    )(
        ensemble,
        control.reshape(members * levels, cols),
        vert_loc,
        obs_source.reshape(1, obs),
        obs_column.reshape(1, obs),
        obs_slot.reshape(1, obs),
        obs_frac.reshape(1, obs),
        obs_count,
    )


def solution(mesh):
    placed = (
        P("member", None, None, "tile"),
        P("member", None, "tile"),
        P(),
        P("tile", None),
        P("tile"),
        P("tile"),
        P("tile"),
        P("tile"),
    )
    return jax.shard_map(
        on_device, mesh=mesh, in_specs=placed, out_specs=P(None, "tile"), check_vma=False
    )
```

profile of v0, /device:TPU:0, one launch (start us, length us, event | category | flops | bytes accessed | tf_op | source)
XLA Modules:
  0.0 18.9 jit_solution(16798717817660324605)
XLA Ops:
  0.7 17.6 %shard_map.82 = f32[32,512]{1,0:T(8,128)S(1)} custom-call(bf16[20,7,32,128]{3,2,1,0:T(8,128)(2,1)} %ens_hbm.1, bf16[640,128]{1,0:T(8,128)(2,1)} %bitcast.5, bf16[32,32]{1,0:T(8,128)(2,1)} %vloc_hbm.1, s32[1,512]{1,0:T(1,128)} %bitcast.6, s32[1,512]{1,0:T(1,128)} %bitcast.7, s32[1,512]{1,0:T(1,128)} %bitcast.8, f32[1,512]{1,0:T(1,128)} %bitcast.9, ...), custom_call_target="tpu_custom_call" | custom-call | tf_op jit(solution)/shard_map/pallas_call | solution.py:284
  18.3 0.6 %copy.10 = f32[32,512]{1,0:T(8,128)} copy(f32[32,512]{1,0:T(8,128)S(1)} %shard_map.82) | data formatting | bytes 131072
where the time goes:
time: 19.1 us; the launch traced here: 18.9 us
  Pallas kernels  17.6 us (92%)
  between operations  0.66 us (3%)
  local copies, waits for them, and re-layouts  0.63 us (3%)
    pallas_call x1, Pallas kernels, on_device(): pl.pallas_call(functools.partial(kernel, tiles, groups, cap, packs), out_...  17.6 us
    unnamed x1, local copies, waits for them, and re-layouts  0.63 us

commit v1 on v0

v1 whole, which is shorter than its diff:
```python
import functools

import jax
import jax.numpy as jnp
from jax import lax
from jax.experimental import pallas as pl
from jax.experimental.pallas import tpu as pltpu
from jax.sharding import PartitionSpec as P

MESH = pl.DeviceIdType.MESH
LANES = 128
F32 = jnp.float32
BF16 = jnp.bfloat16


def iota(shape, axis):
    return lax.broadcasted_iota(jnp.int32, shape, axis)


def one_hot(condition):
    return jnp.where(condition, F32(1.0), F32(0.0)).astype(BF16)


def dot(a, b):
    return jnp.dot(a, b, preferred_element_type=F32)


def dot_nt(a, b):
    return lax.dot_general(a, b, (((1,), (1,)), ((), ())), preferred_element_type=F32)


def two_pieces(x):
    high = x.astype(BF16)
    return high, (x - high.astype(F32)).astype(BF16)


def turned(x, shift):
    shift = shift % LANES
    return x if shift == 0 else pltpu.roll(x, shift, 1)


def kernel(
    tiles, groups, near, cap, packs,
    ens_hbm, ctl_hbm, vloc_hbm, source_hbm, column_hbm, slot_hbm, frac_hbm, count_ref,
    out_ref,
    vloc_ref, source_ref, column_ref, slot_ref, frac_ref, ens, ctl, weighted, part, part_in, asked, relay, req_in, res_out, res_in, place,
    load_sem, part_send, part_recv, near_send, near_recv, far_send, far_recv, res_send, res_recv,
):
    me = lax.axis_index("tile")
    mine = lax.axis_index("member")
    leader = groups - 1
    leads = mine == leader
    members, slots, levels, cols = ens.shape
    rows = levels // packs
    obs = column_ref.shape[1]
    owners = LANES // cap
    far = tiles // near
    low, high = lax.rem(me, near), me // near
    chunk = max(near, owners)
    chunks = tiles // chunk
    lines = chunk // near
    spans = chunk // owners
    width = spans * LANES

    def loaded(index, source, target):
        return pltpu.make_async_copy(source, target, load_sem.at[index])

    loads = [
        loaded(0, source_hbm, source_ref), loaded(1, column_hbm, column_ref),
        loaded(2, slot_hbm, slot_ref), loaded(3, frac_hbm, frac_ref),
        loaded(4, vloc_hbm, vloc_ref), loaded(5, ctl_hbm, ctl), loaded(6, ens_hbm, ens),
    ]

    def near_peer(step):
        return lax.rem(low + step, near)

    def far_peer(step):
        return lax.rem(high + step, far)

    barrier = pltpu.get_barrier_semaphore()

    def greet(tile, member):
        pl.semaphore_signal(
            barrier, inc=1, device_id={"tile": tile, "member": member}, device_id_type=MESH
        )

    @pl.when(leads)
    def _():
        for step in range(1, far):
            greet(far_peer(step) * near + low, leader)
        for step in range(1, near):
            greet(high * near + near_peer(step), leader)
        for member in range(leader):
            greet(me, member)

    @pl.when(jnp.logical_not(leads))
    def _():
        greet(me, leader)

    for load in loads:
        load.start()

    for load in loads[:4]:
        load.wait()
    source = source_ref[...]
    hits = source == iota((tiles, obs), 0)
    hits_f = jnp.where(hits, F32(1.0), F32(0.0))
    before = one_hot(iota((LANES, LANES), 0) < iota((LANES, LANES), 1))
    seen = jnp.zeros((tiles, 1), F32)
    ranks = []
    for block in range(obs // LANES):
        hit = hits_f[:, block * LANES:(block + 1) * LANES]
        ahead = dot(hit.astype(BF16), before) + seen
        ranks.append(jnp.sum(ahead * hit, axis=0, keepdims=True))
        seen = seen + jnp.sum(hit, axis=1, keepdims=True)
    rank = jnp.concatenate(ranks, axis=1).astype(jnp.int32)

    @pl.when(leads)
    def _():
        spread = one_hot(rank == lax.rem(iota((LANES, obs), 0), cap))
        frac = frac_ref[...]
        frac_0 = frac.astype(BF16).astype(F32)
        frac_1 = (frac - frac_0).astype(BF16).astype(F32)
        frac_2 = frac - frac_0 - frac_1
        values = [column_ref[...].astype(F32), slot_ref[...].astype(F32), frac_0, frac_1, frac_2]
        packed = dot_nt(
            jnp.concatenate([jnp.where(hits, v, F32(0.0)) for v in values], axis=0).astype(BF16), spread
        )
        packed = [packed[i * tiles:(i + 1) * tiles] for i in range(len(values))]
        request = jnp.where(
            iota((tiles, LANES), 1) < cap,
            packed[0] + cols * packed[1],
            packed[2] + packed[3] + packed[4],
        )
        for tile in range(tiles):
            asked[tile % near, tile // near] = request[tile:tile + 1]

    batch = max(d for d in range(1, max(1, LANES // levels) + 1) if members % d == 0)
    wide = batch * levels
    repeat = one_hot(lax.rem(iota((wide, levels), 0), levels) == iota((wide, levels), 1))
    for load in loads[4:6]:
        load.wait()
    tall = dot(repeat, vloc_ref[...]).astype(BF16)
    full = dot_nt(tall, repeat)
    factor = jnp.where(
        iota((wide, wide), 0) // levels == iota((wide, wide), 1) // levels, full, F32(0.0)
    ).astype(BF16)
    for step in range(members // batch):
        weighted[step * wide:(step + 1) * wide] = dot(factor, ctl[step * wide:(step + 1) * wide])

    loads[6].wait()
    for slot in range(slots):
        total = jnp.zeros((levels, cols), F32)
        for k in range(members):
            total = total + ens[k, slot].astype(F32) * weighted[k * levels:(k + 1) * levels]
        part[slot * levels:(slot + 1) * levels] = total

    def give(member):
        return pltpu.make_async_remote_copy(
            src_ref=part, dst_ref=part_in.at[member],
            send_sem=part_send, recv_sem=part_recv.at[member],
            device_id={"tile": me, "member": leader}, device_id_type=MESH,
        )

    @pl.when(jnp.logical_not(leads))
    def _():
        pl.semaphore_wait(barrier, 1)
        give(mine).start()

    position = source * cap + rank
    place[...] = one_hot(position == iota((tiles * cap, obs), 0))

    lane = iota((1, LANES), 1)
    stride = jnp.where(2 * me < tiles, 1, chunks - 1)
    home = me // chunk

    def chunk_at(step):
        return lax.rem(home + stride * step, chunks)

    def unless(step, condition, body):
        if step == 0:
            pl.when(condition)(body)
        else:
            body()

    def reply_to(tile, member):
        return pltpu.make_async_remote_copy(
            src_ref=res_out.at[tile], dst_ref=res_in.at[me],
            send_sem=res_send.at[member], recv_sem=res_recv.at[home],
            device_id={"tile": tile, "member": member}, device_id_type=MESH,
        )

    def landed(source, target, send, recv):
        return pltpu.make_async_remote_copy(
            src_ref=source, dst_ref=target, send_sem=send, recv_sem=recv,
            device_id={"tile": me, "member": leader}, device_id_type=MESH,
        )

    @pl.when(leads)
    def _():
        def near_copy(peer, line):
            return pltpu.make_async_remote_copy(
                src_ref=asked.at[peer], dst_ref=relay.at[line],
                send_sem=near_send, recv_sem=near_recv.at[line],
                device_id={"tile": high * near + peer, "member": leader}, device_id_type=MESH,
            )

        def far_copy(peer, line):
            return pltpu.make_async_remote_copy(
                src_ref=relay.at[:, peer], dst_ref=req_in.at[pl.ds(line * near, near)],
                send_sem=far_send, recv_sem=far_recv.at[line],
                device_id={"tile": peer * near + low, "member": leader}, device_id_type=MESH,
            )

        relay[low] = asked[low]
        pl.semaphore_wait(barrier, near + far + groups - 3)
        for step in range(1, near):
            near_copy(near_peer(step), low).start()
        for step in range(1, near):
            near_copy(near_peer(step), near_peer(step)).wait_recv()
        for step in range(1, far):
            far_copy(far_peer(step), high).start()
        req_in[pl.ds(high * near, near)] = relay[:, high]

        increment = part[...]
        for member in range(leader):
            give(member).wait_recv()
            increment = increment + part_in[member]
        pieces = jnp.concatenate(two_pieces(increment), axis=1)

        for step in range(chunks):
            group = chunk_at(step)
            for i in range(lines):
                line = group * lines + i
                unless(step, line != high, lambda line=line: far_copy(line, line).wait_recv())
            codes, fracs = [], []
            for s in range(spans):
                code = jnp.zeros((1, LANES), F32)
                frac = jnp.zeros((1, LANES), F32)
                for i in range(owners):
                    got = req_in[group * chunk + s * owners + i]
                    here = lane // cap == i
                    code = jnp.where(here, turned(got, i * cap), code)
                    frac = jnp.where(here, turned(got, i * cap - cap), frac)
                codes.append(code)
                fracs.append(frac)
            code = jnp.concatenate(codes, axis=1).astype(jnp.int32)
            frac = jnp.concatenate(fracs, axis=1)
            wanted = code // cols
            column = code - wanted * cols
            pick = one_hot(iota((cols, width), 0) == column)
            columns = dot(pieces, jnp.concatenate([pick, pick], axis=0))
            answer = jnp.zeros((levels, width), F32)
            for slot in range(slots):
                weight = jnp.where(
                    wanted == slot, 1.0 - frac, jnp.where(wanted + 1 == slot, frac, F32(0.0))
                )
                answer = answer + weight * columns[slot * levels:(slot + 1) * levels]
            for t in range(chunk):
                s, i = t // owners, t % owners
                tile = group * chunk + t
                packet = jnp.zeros((rows, LANES), F32)
                for j in range(packs):
                    block = answer[j * rows:(j + 1) * rows, s * LANES:(s + 1) * LANES]
                    packet = jnp.where(lane // cap == j, turned(block, (j - i) * cap), packet)
                res_out[tile] = packet
                if step == 0:
                    @pl.when(tile == me)
                    def _():
                        res_in[me] = packet
                unless(step, tile != me, lambda tile=tile: reply_to(tile, leader).start())
                for member in range(leader):
                    reply_to(tile, member).start()

    both = jnp.zeros((2 * levels, obs), F32)
    for step in range(chunks):
        group = chunk_at(step)
        whole = res_in.at[pl.ds(group * chunk, chunk)]
        if step == 0:
            if chunk > 1:
                @pl.when(leads)
                def _():
                    rest = res_in.at[pl.ds(0, chunk - 1)]
                    landed(rest, rest, res_send.at[leader], res_recv.at[group]).wait_recv()

            @pl.when(jnp.logical_not(leads))
            def _():
                landed(whole, whole, res_send.at[leader], res_recv.at[group]).wait_recv()
        else:
            landed(whole, whole, res_send.at[leader], res_recv.at[group]).wait_recv()
        columns = []
        for s in range(spans):
            bands = [jnp.zeros((rows, LANES), F32)] * packs
            for i in range(owners):
                got = res_in[group * chunk + s * owners + i]
                for j in range(packs):
                    bands[j] = jnp.where(lane // cap == i, turned(got, (i - j) * cap), bands[j])
            columns.append(jnp.concatenate(bands, axis=0))
        upper, lower = two_pieces(jnp.concatenate(columns, axis=1))
        first = pl.multiple_of(group * width, LANES)
        both = both + dot(jnp.concatenate([upper, lower], axis=0), place[pl.ds(first, width)])
    live = iota((levels, obs), 1) < count_ref[0]
    out_ref[...] = jnp.where(live, both[:levels] + both[levels:], F32(0.0))

    @pl.when(jnp.logical_not(leads))
    def _():
        give(mine).wait_send()

    @pl.when(leads)
    def _():
        def sent(buffer, sem):
            landed(buffer, buffer, sem, far_recv.at[0]).wait_send()

        if near > 1:
            sent(asked.at[pl.ds(0, near - 1)], near_send)
        if far > 1:
            sent(req_in.at[pl.ds(0, (far - 1) * near)], far_send)
        for member in range(leader):
            sent(res_out, res_send.at[member])
        if tiles > 1:
            sent(res_out.at[pl.ds(0, tiles - 1)], res_send.at[leader])


def on_device(ensemble, control, vert_loc, obs_source, obs_column, obs_slot, obs_frac, obs_count):
    tiles, groups = lax.axis_size("tile"), lax.axis_size("member")
    members, slots, levels, cols = ensemble.shape
    obs = obs_column.shape[0]
    cap = max(4, 2 * obs // tiles)
    near = max(d for d in range(1, tiles + 1) if tiles % d == 0 and d * d <= tiles)
    packs = max(1, min(LANES // cap, levels // 8))
    rows = levels // packs
    chunks = tiles // max(near, LANES // cap)
    vmem = pl.BlockSpec(memory_space=pltpu.VMEM)
    hbm = pl.BlockSpec(memory_space=pl.ANY)
    dma = pltpu.SemaphoreType.DMA
    return pl.pallas_call(
        functools.partial(kernel, tiles, groups, near, cap, packs),
        out_shape=pltpu.VMEM((levels, obs), F32),
        in_specs=[hbm] * 7 + [pl.BlockSpec(memory_space=pltpu.SMEM)],
        out_specs=vmem,
        scratch_shapes=[
            pltpu.VMEM((levels, levels), BF16),
            pltpu.VMEM((1, obs), jnp.int32),
            pltpu.VMEM((1, obs), jnp.int32),
            pltpu.VMEM((1, obs), jnp.int32),
            pltpu.VMEM((1, obs), F32),
            pltpu.VMEM((members, slots, levels, cols), BF16),
            pltpu.VMEM((members * levels, cols), BF16),
            pltpu.VMEM((members * levels, cols), F32),
            pltpu.VMEM((slots * levels, cols), F32),
            pltpu.VMEM((max(1, groups - 1), slots * levels, cols), F32),
            pltpu.VMEM((near, tiles // near, 1, LANES), F32),
            pltpu.VMEM((near, tiles // near, 1, LANES), F32),
            pltpu.VMEM((tiles, 1, LANES), F32),
            pltpu.VMEM((tiles, rows, LANES), F32),
            pltpu.VMEM((tiles, rows, LANES), F32),
            pltpu.VMEM((tiles * cap, obs), BF16),
            dma((7,)),
            dma,
            dma((max(1, groups - 1),)),
            dma,
            dma((near,)),
            dma,
            dma((tiles // near,)),
            dma((groups,)),
            dma((chunks,)),
        ],
        compiler_params=pltpu.CompilerParams(collective_id=0, has_side_effects=True),
    )(
        ensemble,
        control.reshape(members * levels, cols),
        vert_loc,
        obs_source.reshape(1, obs),
        obs_column.reshape(1, obs),
        obs_slot.reshape(1, obs),
        obs_frac.reshape(1, obs),
        obs_count,
    )


def solution(mesh):
    placed = (
        P("member", None, None, "tile"),
        P("member", None, "tile"),
        P(),
        P("tile", None),
        P("tile"),
        P("tile"),
        P("tile"),
        P("tile"),
    )
    return jax.shard_map(
        on_device, mesh=mesh, in_specs=placed, out_specs=P(None, "tile"), check_vma=False
    )
```

time: 19.1 us -> 16.2 us (0.85)
  Pallas kernels: 17.6 us -> 14.8 us
    pallas_call x1, Pallas kernels: 17.6 us -> 14.8 us  [on_device(): pl.pallas_call(functools.partial(kernel, tiles, groups, near, cap, packs)...]
where the time goes in v1:
time: 16.2 us; the launch traced here: 16 us
  Pallas kernels  14.8 us (91%)
  between operations  0.66 us (4%)
  local copies, waits for them, and re-layouts  0.63 us (4%)
    pallas_call x1, Pallas kernels, on_device(): pl.pallas_call(functools.partial(kernel, tiles, groups, near, cap, packs)...  14.8 us
    unnamed x1, local copies, waits for them, and re-layouts  0.63 us

profile of v1, /device:TPU:0, one launch (start us, length us, event | category | flops | bytes accessed | tf_op | source)
XLA Modules:
  0.0 16.0 jit_solution(12460758157021907034)
XLA Ops:
  0.7 14.8 %shard_map.82 = f32[32,512]{1,0:T(8,128)S(1)} custom-call(bf16[20,7,32,128]{3,2,1,0:T(8,128)(2,1)} %ens_hbm.1, bf16[640,128]{1,0:T(8,128)(2,1)} %bitcast.5, bf16[32,32]{1,0:T(8,128)(2,1)} %vloc_hbm.1, s32[1,512]{1,0:T(1,128)} %bitcast.6, s32[1,512]{1,0:T(1,128)} %bitcast.7, s32[1,512]{1,0:T(1,128)} %bitcast.8, f32[1,512]{1,0:T(1,128)} %bitcast.9, ...), custom_call_target="tpu_custom_call" | custom-call | tf_op jit(solution)/shard_map/pallas_call | solution.py:336
  15.4 0.6 %copy.10 = f32[32,512]{1,0:T(8,128)} copy(f32[32,512]{1,0:T(8,128)S(1)} %shard_map.82) | data formatting | bytes 131072

commit v2 on v1

--- a/solution.py
+++ b/solution.py
@@ -44,11 +44,12 @@
     ens_hbm, ctl_hbm, vloc_hbm, source_hbm, column_hbm, slot_hbm, frac_hbm, count_ref,
     out_ref,
     vloc_ref, source_ref, column_ref, slot_ref, frac_ref, ens, ctl, weighted, part, part_in, asked, relay, req_in, res_out, res_in, place,
-    load_sem, part_send, part_recv, near_send, near_recv, far_send, far_recv, res_send, res_recv,
+    load_sem, far_in, part_send, part_recv, near_send, near_recv, far_send, far_recv, res_send, res_recv,
 ):
     me = lax.axis_index("tile")
     mine = lax.axis_index("member")
     leader = groups - 1
+    collector = leader - 1
     leads = mine == leader
     members, slots, levels, cols = ens.shape
     rows = levels // packs
@@ -86,8 +87,8 @@
 
     @pl.when(leads)
     def _():
-        for step in range(1, far):
-            greet(far_peer(step) * near + low, leader)
+        for step in range(far - 1, 0, -1):
+            greet(far_peer(step) * near + low, collector)
         for step in range(1, near):
             greet(high * near + near_peer(step), leader)
         for member in range(leader):
@@ -100,23 +101,34 @@
     for load in loads:
         load.start()
 
+    def near_copy(peer, line):
+        return pltpu.make_async_remote_copy(
+            src_ref=asked.at[peer], dst_ref=relay.at[line],
+            send_sem=near_send, recv_sem=near_recv.at[line],
+            device_id={"tile": high * near + peer, "member": leader}, device_id_type=MESH,
+        )
+
+    def ranked():
+        source = source_ref[...]
+        hits = source == iota((tiles, obs), 0)
+        hits_f = jnp.where(hits, F32(1.0), F32(0.0))
+        before = one_hot(iota((LANES, LANES), 0) < iota((LANES, LANES), 1))
+        seen = jnp.zeros((tiles, 1), F32)
+        ranks = []
+        for block in range(obs // LANES):
+            hit = hits_f[:, block * LANES:(block + 1) * LANES]
+            ahead = dot(hit.astype(BF16), before) + seen
+            ranks.append(jnp.sum(ahead * hit, axis=0, keepdims=True))
+            seen = seen + jnp.sum(hit, axis=1, keepdims=True)
+        rank = jnp.concatenate(ranks, axis=1).astype(jnp.int32)
+        return source, hits, rank
+
     for load in loads[:4]:
         load.wait()
-    source = source_ref[...]
-    hits = source == iota((tiles, obs), 0)
-    hits_f = jnp.where(hits, F32(1.0), F32(0.0))
-    before = one_hot(iota((LANES, LANES), 0) < iota((LANES, LANES), 1))
-    seen = jnp.zeros((tiles, 1), F32)
-    ranks = []
-    for block in range(obs // LANES):
-        hit = hits_f[:, block * LANES:(block + 1) * LANES]
-        ahead = dot(hit.astype(BF16), before) + seen
-        ranks.append(jnp.sum(ahead * hit, axis=0, keepdims=True))
-        seen = seen + jnp.sum(hit, axis=1, keepdims=True)
-    rank = jnp.concatenate(ranks, axis=1).astype(jnp.int32)
 
     @pl.when(leads)
     def _():
+        source, hits, rank = ranked()
         spread = one_hot(rank == lax.rem(iota((LANES, obs), 0), cap))
         frac = frac_ref[...]
         frac_0 = frac.astype(BF16).astype(F32)
@@ -127,13 +139,17 @@
             jnp.concatenate([jnp.where(hits, v, F32(0.0)) for v in values], axis=0).astype(BF16), spread
         )
         packed = [packed[i * tiles:(i + 1) * tiles] for i in range(len(values))]
-        request = jnp.where(
-            iota((tiles, LANES), 1) < cap,
-            packed[0] + cols * packed[1],
-            packed[2] + packed[3] + packed[4],
-        )
+        seat = iota((tiles, LANES), 1) // cap == lax.rem(me, owners)
+        code = jnp.where(seat, packed[0] + cols * packed[1], F32(0.0))
+        part_of = jnp.where(seat, packed[2] + packed[3] + packed[4], F32(0.0))
         for tile in range(tiles):
-            asked[tile % near, tile // near] = request[tile:tile + 1]
+            asked[tile % near, tile // near, 0:1] = code[tile:tile + 1]
+            asked[tile % near, tile // near, 1:2] = part_of[tile:tile + 1]
+        place[...] = one_hot(source * cap + rank == iota((tiles * cap, obs), 0))
+        pl.semaphore_wait(barrier, near + groups - 2)
+        for step in range(1, near):
+            near_copy(near_peer(step), low).start()
+        relay[low] = asked[low]
 
     batch = max(d for d in range(1, max(1, LANES // levels) + 1) if members % d == 0)
     wide = batch * levels
@@ -164,11 +180,18 @@
 
     @pl.when(jnp.logical_not(leads))
     def _():
-        pl.semaphore_wait(barrier, 1)
+        gathers = mine == collector
+        pl.semaphore_wait(barrier, jnp.where(gathers, far, 1))
         give(mine).start()
 
-    position = source * cap + rank
-    place[...] = one_hot(position == iota((tiles * cap, obs), 0))
+        @pl.when(gathers)
+        def _():
+            pl.semaphore_signal(
+                far_in, inc=1, device_id={"tile": me, "member": leader}, device_id_type=MESH
+            )
+
+        source, _, rank = ranked()
+        place[...] = one_hot(source * cap + rank == iota((tiles * cap, obs), 0))
 
     lane = iota((1, LANES), 1)
     stride = jnp.where(2 * me < tiles, 1, chunks - 1)
@@ -176,6 +199,9 @@
 
     def chunk_at(step):
         return lax.rem(home + stride * step, chunks)
+
+    def served(step):
+        return home if step == 0 else jnp.where(step - 1 < home, step - 1, step)
 
     def unless(step, condition, body):
         if step == 0:
@@ -198,13 +224,6 @@
 
     @pl.when(leads)
     def _():
-        def near_copy(peer, line):
-            return pltpu.make_async_remote_copy(
-                src_ref=asked.at[peer], dst_ref=relay.at[line],
-                send_sem=near_send, recv_sem=near_recv.at[line],
-                device_id={"tile": high * near + peer, "member": leader}, device_id_type=MESH,
-            )
-
         def far_copy(peer, line):
             return pltpu.make_async_remote_copy(
                 src_ref=relay.at[:, peer], dst_ref=req_in.at[pl.ds(line * near, near)],
@@ -212,12 +231,9 @@
                 device_id={"tile": peer * near + low, "member": leader}, device_id_type=MESH,
             )
 
-        relay[low] = asked[low]
-        pl.semaphore_wait(barrier, near + far + groups - 3)
-        for step in range(1, near):
-            near_copy(near_peer(step), low).start()
         for step in range(1, near):
             near_copy(near_peer(step), near_peer(step)).wait_recv()
+        pl.semaphore_wait(far_in, 1)
         for step in range(1, far):
             far_copy(far_peer(step), high).start()
         req_in[pl.ds(high * near, near)] = relay[:, high]
@@ -229,19 +245,17 @@
         pieces = jnp.concatenate(two_pieces(increment), axis=1)
 
         for step in range(chunks):
-            group = chunk_at(step)
+            group = served(step)
             for i in range(lines):
                 line = group * lines + i
                 unless(step, line != high, lambda line=line: far_copy(line, line).wait_recv())
             codes, fracs = [], []
             for s in range(spans):
-                code = jnp.zeros((1, LANES), F32)
-                frac = jnp.zeros((1, LANES), F32)
-                for i in range(owners):
-                    got = req_in[group * chunk + s * owners + i]
-                    here = lane // cap == i
-                    code = jnp.where(here, turned(got, i * cap), code)
-                    frac = jnp.where(here, turned(got, i * cap - cap), frac)
+                first = group * chunk + s * owners
+                code, frac = req_in[first, 0:1], req_in[first, 1:2]
+                for i in range(1, owners):
+                    code = code + req_in[first + i, 0:1]
+                    frac = frac + req_in[first + i, 1:2]
                 codes.append(code)
                 fracs.append(frac)
             code = jnp.concatenate(codes, axis=1).astype(jnp.int32)
@@ -268,9 +282,11 @@
                     @pl.when(tile == me)
                     def _():
                         res_in[me] = packet
-                unless(step, tile != me, lambda tile=tile: reply_to(tile, leader).start())
                 for member in range(leader):
                     reply_to(tile, member).start()
+            for t in range(chunk):
+                tile = group * chunk + t
+                unless(step, tile != me, lambda tile=tile: reply_to(tile, leader).start())
 
     both = jnp.zeros((2 * levels, obs), F32)
     for step in range(chunks):
@@ -349,13 +365,14 @@
             pltpu.VMEM((members * levels, cols), F32),
             pltpu.VMEM((slots * levels, cols), F32),
             pltpu.VMEM((max(1, groups - 1), slots * levels, cols), F32),
-            pltpu.VMEM((near, tiles // near, 1, LANES), F32),
-            pltpu.VMEM((near, tiles // near, 1, LANES), F32),
-            pltpu.VMEM((tiles, 1, LANES), F32),
+            pltpu.VMEM((near, tiles // near, 2, LANES), F32),
+            pltpu.VMEM((near, tiles // near, 2, LANES), F32),
+            pltpu.VMEM((tiles, 2, LANES), F32),
             pltpu.VMEM((tiles, rows, LANES), F32),
             pltpu.VMEM((tiles, rows, LANES), F32),
             pltpu.VMEM((tiles * cap, obs), BF16),
             dma((7,)),
+            pltpu.SemaphoreType.REGULAR,
             dma,
             dma((max(1, groups - 1),)),
             dma,

time: 16.2 us -> 14.8 us (0.914)
  Pallas kernels: 14.8 us -> 13.4 us
    pallas_call x1, Pallas kernels: 14.8 us -> 13.4 us  [on_device(): pl.pallas_call(functools.partial(kernel, tiles, groups, near, cap, packs)...]
where the time goes in v2:
time: 14.8 us; the launch traced here: 14.7 us
  Pallas kernels  13.4 us (91%)
  between operations  0.66 us (4%)
  local copies, waits for them, and re-layouts  0.63 us (4%)
    pallas_call x1, Pallas kernels, on_device(): pl.pallas_call(functools.partial(kernel, tiles, groups, near, cap, packs)...  13.4 us
    unnamed x1, local copies, waits for them, and re-layouts  0.63 us

profile of v2, /device:TPU:0, one launch (start us, length us, event | category | flops | bytes accessed | tf_op | source)
XLA Modules:
  0.0 14.7 jit_solution(13069945156018045713)
XLA Ops:
  0.7 13.4 %shard_map.82 = f32[32,512]{1,0:T(8,128)S(1)} custom-call(bf16[20,7,32,128]{3,2,1,0:T(8,128)(2,1)} %ens_hbm.1, bf16[640,128]{1,0:T(8,128)(2,1)} %bitcast.5, bf16[32,32]{1,0:T(8,128)(2,1)} %vloc_hbm.1, s32[1,512]{1,0:T(1,128)} %bitcast.6, s32[1,512]{1,0:T(1,128)} %bitcast.7, s32[1,512]{1,0:T(1,128)} %bitcast.8, f32[1,512]{1,0:T(1,128)} %bitcast.9, ...), custom_call_target="tpu_custom_call" | custom-call | tf_op jit(solution)/shard_map/pallas_call | solution.py:352
  14.0 0.6 %copy.10 = f32[32,512]{1,0:T(8,128)} copy(f32[32,512]{1,0:T(8,128)S(1)} %shard_map.82) | data formatting | bytes 131072

commit v3 on v2

--- a/solution.py
+++ b/solution.py
@@ -44,7 +44,8 @@
     ens_hbm, ctl_hbm, vloc_hbm, source_hbm, column_hbm, slot_hbm, frac_hbm, count_ref,
     out_ref,
     vloc_ref, source_ref, column_ref, slot_ref, frac_ref, ens, ctl, weighted, part, part_in, asked, relay, req_in, res_out, res_in, place,
-    load_sem, far_in, part_send, part_recv, near_send, near_recv, far_send, far_recv, res_send, res_recv,
+    rest_in, part_recv, near_recv, far_recv, res_recv,
+    load_sem, part_send, near_send, far_send, res_send,
 ):
     me = lax.axis_index("tile")
     mine = lax.axis_index("member")
@@ -85,18 +86,21 @@
             barrier, inc=1, device_id={"tile": tile, "member": member}, device_id_type=MESH
         )
 
+    def taker(digit, direct):
+        return jnp.where((digit == 0) == direct, leader, collector)
+
     @pl.when(leads)
     def _():
-        for step in range(far - 1, 0, -1):
-            greet(far_peer(step) * near + low, collector)
-        for step in range(1, near):
-            greet(high * near + near_peer(step), leader)
+        for step in range(1, far):
+            greet(far_peer(step) * near + low, taker(low, False))
+        for step in range(near - 1, 0, -1):
+            greet(high * near + near_peer(step), taker(near_peer(step), True))
         for member in range(leader):
             greet(me, member)
 
-    @pl.when(jnp.logical_not(leads))
-    def _():
-        greet(me, leader)
+    @pl.when(jnp.logical_not(leads) & ((mine != collector) | (low == 0)))
+    def _():
+        greet(me, taker(low, True))
 
     for load in loads:
         load.start()
@@ -145,11 +149,29 @@
         for tile in range(tiles):
             asked[tile % near, tile // near, 0:1] = code[tile:tile + 1]
             asked[tile % near, tile // near, 1:2] = part_of[tile:tile + 1]
-        place[...] = one_hot(source * cap + rank == iota((tiles * cap, obs), 0))
-        pl.semaphore_wait(barrier, near + groups - 2)
+
+        @pl.when(low == 0)
+        def _():
+            pl.semaphore_wait(barrier, near + groups - 2)
+
+        @pl.when(low != 0)
+        def _():
+            pl.semaphore_wait(rest_in, 1)
+
         for step in range(1, near):
             near_copy(near_peer(step), low).start()
         relay[low] = asked[low]
+        place[...] = one_hot(source * cap + rank == iota((tiles * cap, obs), 0))
+
+    def entered(count):
+        pl.semaphore_wait(barrier, count)
+        pl.semaphore_signal(
+            rest_in, inc=1, device_id={"tile": me, "member": leader}, device_id_type=MESH
+        )
+
+    @pl.when((mine == collector) & (low != 0))
+    def _():
+        entered(near + groups - 2)
 
     batch = max(d for d in range(1, max(1, LANES // levels) + 1) if members % d == 0)
     wide = batch * levels
@@ -180,16 +202,15 @@
 
     @pl.when(jnp.logical_not(leads))
     def _():
-        gathers = mine == collector
-        pl.semaphore_wait(barrier, jnp.where(gathers, far, 1))
+        @pl.when((mine == collector) & (low == 0))
+        def _():
+            entered(far)
+
+        @pl.when(mine != collector)
+        def _():
+            pl.semaphore_wait(barrier, 1)
+
         give(mine).start()
-
-        @pl.when(gathers)
-        def _():
-            pl.semaphore_signal(
-                far_in, inc=1, device_id={"tile": me, "member": leader}, device_id_type=MESH
-            )
-
         source, _, rank = ranked()
         place[...] = one_hot(source * cap + rank == iota((tiles * cap, obs), 0))
 
@@ -233,7 +254,15 @@
 
         for step in range(1, near):
             near_copy(near_peer(step), near_peer(step)).wait_recv()
-        pl.semaphore_wait(far_in, 1)
+
+        @pl.when(low == 0)
+        def _():
+            pl.semaphore_wait(rest_in, 1)
+
+        @pl.when(low != 0)
+        def _():
+            pl.semaphore_wait(barrier, far - 1)
+
         for step in range(1, far):
             far_copy(far_peer(step), high).start()
         req_in[pl.ds(high * near, near)] = relay[:, high]
@@ -337,6 +366,13 @@
             sent(res_out.at[pl.ds(0, tiles - 1)], res_send.at[leader])
 
 
+def scoped(*args):
+    dma = pltpu.SemaphoreType.DMA
+    pl.run_scoped(
+        functools.partial(kernel, *args), dma((7,)), dma(()), dma(()), dma(()), dma((args[1],))
+    )
+
+
 def on_device(ensemble, control, vert_loc, obs_source, obs_column, obs_slot, obs_frac, obs_count):
     tiles, groups = lax.axis_size("tile"), lax.axis_size("member")
     members, slots, levels, cols = ensemble.shape
@@ -350,7 +386,7 @@
     hbm = pl.BlockSpec(memory_space=pl.ANY)
     dma = pltpu.SemaphoreType.DMA
     return pl.pallas_call(
-        functools.partial(kernel, tiles, groups, near, cap, packs),
+        functools.partial(scoped, tiles, groups, near, cap, packs),
         out_shape=pltpu.VMEM((levels, obs), F32),
         in_specs=[hbm] * 7 + [pl.BlockSpec(memory_space=pltpu.SMEM)],
         out_specs=vmem,
@@ -371,15 +407,10 @@
             pltpu.VMEM((tiles, rows, LANES), F32),
             pltpu.VMEM((tiles, rows, LANES), F32),
             pltpu.VMEM((tiles * cap, obs), BF16),
-            dma((7,)),
             pltpu.SemaphoreType.REGULAR,
-            dma,
             dma((max(1, groups - 1),)),
-            dma,
             dma((near,)),
-            dma,
             dma((tiles // near,)),
-            dma((groups,)),
             dma((chunks,)),
         ],
         compiler_params=pltpu.CompilerParams(collective_id=0, has_side_effects=True),

time: 14.8 us -> 14.5 us (0.980)
  Pallas kernels: 13.4 us -> 13 us
    pallas_call x1, Pallas kernels: 13.4 us -> 13 us  [on_device(): pl.pallas_call(functools.partial(scoped, tiles, groups, near, cap, packs)...]
where the time goes in v3:
time: 14.5 us; the launch traced here: 14.3 us
  Pallas kernels  13 us (90%)
  between operations  0.66 us (5%)
  local copies, waits for them, and re-layouts  0.63 us (4%)
    pallas_call x1, Pallas kernels, on_device(): pl.pallas_call(functools.partial(scoped, tiles, groups, near, cap, packs)...  13 us
    unnamed x1, local copies, waits for them, and re-layouts  0.63 us

profile of v3, /device:TPU:0, one launch (start us, length us, event | category | flops | bytes accessed | tf_op | source)
XLA Modules:
  0.0 14.3 jit_solution(9144029780295872593)
XLA Ops:
  0.7 13.0 %shard_map.82 = f32[32,512]{1,0:T(8,128)S(1)} custom-call(bf16[20,7,32,128]{3,2,1,0:T(8,128)(2,1)} %args_0_.4, bf16[640,128]{1,0:T(8,128)(2,1)} %bitcast.5, bf16[32,32]{1,0:T(8,128)(2,1)} %args_2_.4, s32[1,512]{1,0:T(1,128)} %bitcast.6, s32[1,512]{1,0:T(1,128)} %bitcast.7, s32[1,512]{1,0:T(1,128)} %bitcast.8, f32[1,512]{1,0:T(1,128)} %bitcast.9, ...), custom_call_target="tpu_custom_call" | custom-call | tf_op jit(solution)/shard_map/pallas_call | solution.py:388
  13.7 0.6 %copy.10 = f32[32,512]{1,0:T(8,128)} copy(f32[32,512]{1,0:T(8,128)S(1)} %shard_map.82) | data formatting | bytes 131072

commit v4 on v3

--- a/solution.py
+++ b/solution.py
@@ -91,10 +91,10 @@
 
     @pl.when(leads)
     def _():
+        for step in range(1, near):
+            greet(high * near + near_peer(step), taker(near_peer(step), True))
         for step in range(1, far):
             greet(far_peer(step) * near + low, taker(low, False))
-        for step in range(near - 1, 0, -1):
-            greet(high * near + near_peer(step), taker(near_peer(step), True))
         for member in range(leader):
             greet(me, member)
 
@@ -108,7 +108,7 @@
     def near_copy(peer, line):
         return pltpu.make_async_remote_copy(
             src_ref=asked.at[peer], dst_ref=relay.at[line],
-            send_sem=near_send, recv_sem=near_recv.at[line],
+            send_sem=near_send, recv_sem=near_recv,
             device_id={"tile": high * near + peer, "member": leader}, device_id_type=MESH,
         )
 
@@ -127,6 +127,11 @@
         rank = jnp.concatenate(ranks, axis=1).astype(jnp.int32)
         return source, hits, rank
 
+    def placed(source, rank):
+        live = iota((1, obs), 1) < count_ref[0]
+        position = jnp.where(live, source * cap + rank, -1)
+        return one_hot(position == iota((tiles * cap, obs), 0))
+
     for load in loads[:4]:
         load.wait()
 
@@ -161,7 +166,7 @@
         for step in range(1, near):
             near_copy(near_peer(step), low).start()
         relay[low] = asked[low]
-        place[...] = one_hot(source * cap + rank == iota((tiles * cap, obs), 0))
+        place[...] = placed(source, rank)
 
     def entered(count):
         pl.semaphore_wait(barrier, count)
@@ -212,7 +217,7 @@
 
         give(mine).start()
         source, _, rank = ranked()
-        place[...] = one_hot(source * cap + rank == iota((tiles * cap, obs), 0))
+        place[...] = placed(source, rank)
 
     lane = iota((1, LANES), 1)
     stride = jnp.where(2 * me < tiles, 1, chunks - 1)
@@ -252,8 +257,9 @@
                 device_id={"tile": peer * near + low, "member": leader}, device_id_type=MESH,
             )
 
-        for step in range(1, near):
-            near_copy(near_peer(step), near_peer(step)).wait_recv()
+        if near > 1:
+            others = relay.at[pl.ds(0, near - 1)]
+            landed(others, others, near_send, near_recv).wait_recv()
 
         @pl.when(low == 0)
         def _():
@@ -344,8 +350,7 @@
         upper, lower = two_pieces(jnp.concatenate(columns, axis=1))
         first = pl.multiple_of(group * width, LANES)
         both = both + dot(jnp.concatenate([upper, lower], axis=0), place[pl.ds(first, width)])
-    live = iota((levels, obs), 1) < count_ref[0]
-    out_ref[...] = jnp.where(live, both[:levels] + both[levels:], F32(0.0))
+    out_ref[...] = both[:levels] + both[levels:]
 
     @pl.when(jnp.logical_not(leads))
     def _():
@@ -366,10 +371,13 @@
             sent(res_out.at[pl.ds(0, tiles - 1)], res_send.at[leader])
 
 
-def scoped(*args):
+def scoped(tiles, groups, near, cap, packs, *refs):
     dma = pltpu.SemaphoreType.DMA
+    one, chunks = dma(()), tiles // max(near, LANES // cap)
     pl.run_scoped(
-        functools.partial(kernel, *args), dma((7,)), dma(()), dma(()), dma(()), dma((args[1],))
+        functools.partial(kernel, tiles, groups, near, cap, packs, *refs),
+        pltpu.SemaphoreType.REGULAR(()), dma((max(1, groups - 1),)), one, dma((tiles // near,)), dma((chunks,)),
+        dma((7,)), one, one, one, dma((groups,)),
     )
 
 
@@ -381,10 +389,8 @@
     near = max(d for d in range(1, tiles + 1) if tiles % d == 0 and d * d <= tiles)
     packs = max(1, min(LANES // cap, levels // 8))
     rows = levels // packs
-    chunks = tiles // max(near, LANES // cap)
     vmem = pl.BlockSpec(memory_space=pltpu.VMEM)
     hbm = pl.BlockSpec(memory_space=pl.ANY)
-    dma = pltpu.SemaphoreType.DMA
     return pl.pallas_call(
         functools.partial(scoped, tiles, groups, near, cap, packs),
         out_shape=pltpu.VMEM((levels, obs), F32),
@@ -407,11 +413,6 @@
             pltpu.VMEM((tiles, rows, LANES), F32),
             pltpu.VMEM((tiles, rows, LANES), F32),
             pltpu.VMEM((tiles * cap, obs), BF16),
-            pltpu.SemaphoreType.REGULAR,
-            dma((max(1, groups - 1),)),
-            dma((near,)),
-            dma((tiles // near,)),
-            dma((chunks,)),
         ],
         compiler_params=pltpu.CompilerParams(collective_id=0, has_side_effects=True),
     )(

time: 14.5 us -> 14.3 us (0.986)
  Pallas kernels: 13 us -> 12.8 us
    pallas_call x1, Pallas kernels: 13 us -> 12.8 us  [on_device(): pl.pallas_call(functools.partial(scoped, tiles, groups, near, cap, packs)...]
where the time goes in v4:
time: 14.3 us; the launch traced here: 14.1 us
  Pallas kernels  12.8 us (90%)
  local copies, waits for them, and re-layouts  0.65 us (5%)
  between operations  0.65 us (5%)
    pallas_call x1, Pallas kernels, on_device(): pl.pallas_call(functools.partial(scoped, tiles, groups, near, cap, packs)...  12.8 us
    unnamed x1, local copies, waits for them, and re-layouts  0.65 us

profile of v4, /device:TPU:0, one launch (start us, length us, event | category | flops | bytes accessed | tf_op | source)
XLA Modules:
  0.0 14.1 jit_solution(4545763403054112704)
XLA Ops:
  0.7 12.8 %shard_map.82 = f32[32,512]{1,0:T(8,128)S(1)} custom-call(bf16[20,7,32,128]{3,2,1,0:T(8,128)(2,1)} %refs_0_.1, bf16[640,128]{1,0:T(8,128)(2,1)} %bitcast.5, bf16[32,32]{1,0:T(8,128)(2,1)} %refs_2_.1, s32[1,512]{1,0:T(1,128)} %bitcast.6, s32[1,512]{1,0:T(1,128)} %bitcast.7, s32[1,512]{1,0:T(1,128)} %bitcast.8, f32[1,512]{1,0:T(1,128)} %bitcast.9, ...), custom_call_target="tpu_custom_call" | custom-call | tf_op jit(solution)/shard_map/pallas_call | solution.py:394
  13.4 0.7 %copy.10 = f32[32,512]{1,0:T(8,128)} copy(f32[32,512]{1,0:T(8,128)S(1)} %shard_map.82) | data formatting | bytes 131072

commit v5 on v4

--- a/solution.py
+++ b/solution.py
@@ -163,7 +163,7 @@
         def _():
             pl.semaphore_wait(rest_in, 1)
 
-        for step in range(1, near):
+        for step in range(near - 1, 0, -1):
             near_copy(near_peer(step), low).start()
         relay[low] = asked[low]
         place[...] = placed(source, rank)
@@ -269,7 +269,7 @@
         def _():
             pl.semaphore_wait(barrier, far - 1)
 
-        for step in range(1, far):
+        for step in range(far - 1, 0, -1):
             far_copy(far_peer(step), high).start()
         req_in[pl.ds(high * near, near)] = relay[:, high]
 
@@ -284,33 +284,30 @@
             for i in range(lines):
                 line = group * lines + i
                 unless(step, line != high, lambda line=line: far_copy(line, line).wait_recv())
-            codes, fracs = [], []
+            answers = []
             for s in range(spans):
                 first = group * chunk + s * owners
                 code, frac = req_in[first, 0:1], req_in[first, 1:2]
                 for i in range(1, owners):
                     code = code + req_in[first + i, 0:1]
                     frac = frac + req_in[first + i, 1:2]
-                codes.append(code)
-                fracs.append(frac)
-            code = jnp.concatenate(codes, axis=1).astype(jnp.int32)
-            frac = jnp.concatenate(fracs, axis=1)
-            wanted = code // cols
-            column = code - wanted * cols
-            pick = one_hot(iota((cols, width), 0) == column)
-            columns = dot(pieces, jnp.concatenate([pick, pick], axis=0))
-            answer = jnp.zeros((levels, width), F32)
-            for slot in range(slots):
-                weight = jnp.where(
-                    wanted == slot, 1.0 - frac, jnp.where(wanted + 1 == slot, frac, F32(0.0))
-                )
-                answer = answer + weight * columns[slot * levels:(slot + 1) * levels]
+                wanted = jnp.floor((code + 0.5) * (1.0 / cols))
+                column = (code - cols * wanted).astype(jnp.int32)
+                pick = one_hot(iota((cols, LANES), 0) == column)
+                columns = dot(pieces, jnp.concatenate([pick, pick], axis=0))
+                answer = jnp.zeros((levels, LANES), F32)
+                for slot in range(slots):
+                    weight = jnp.where(
+                        wanted == slot, 1.0 - frac, jnp.where(wanted == slot - 1, frac, F32(0.0))
+                    )
+                    answer = answer + weight * columns[slot * levels:(slot + 1) * levels]
+                answers.append(answer)
             for t in range(chunk):
                 s, i = t // owners, t % owners
                 tile = group * chunk + t
                 packet = jnp.zeros((rows, LANES), F32)
                 for j in range(packs):
-                    block = answer[j * rows:(j + 1) * rows, s * LANES:(s + 1) * LANES]
+                    block = answers[s][j * rows:(j + 1) * rows]
                     packet = jnp.where(lane // cap == j, turned(block, (j - i) * cap), packet)
                 res_out[tile] = packet
                 if step == 0:

time: 14.3 us -> 14.1 us (0.986)
  Pallas kernels: 12.8 us -> 12.6 us
where the time goes in v5:
time: 14.1 us; the launch traced here: 14 us
  Pallas kernels  12.6 us (89%)
  local copies, waits for them, and re-layouts  0.65 us (5%)
  between operations  0.65 us (5%)
    pallas_call x1, Pallas kernels, on_device(): pl.pallas_call(functools.partial(scoped, tiles, groups, near, cap, packs)...  12.6 us
    unnamed x1, local copies, waits for them, and re-layouts  0.65 us

profile of v5, /device:TPU:0, one launch (start us, length us, event | category | flops | bytes accessed | tf_op | source)
XLA Modules:
  0.0 14.0 jit_solution(14693225652955384167)
XLA Ops:
  0.7 12.6 %shard_map.82 = f32[32,512]{1,0:T(8,128)S(1)} custom-call(bf16[20,7,32,128]{3,2,1,0:T(8,128)(2,1)} %refs_0_.1, bf16[640,128]{1,0:T(8,128)(2,1)} %bitcast.5, bf16[32,32]{1,0:T(8,128)(2,1)} %refs_2_.1, s32[1,512]{1,0:T(1,128)} %bitcast.6, s32[1,512]{1,0:T(1,128)} %bitcast.7, s32[1,512]{1,0:T(1,128)} %bitcast.8, f32[1,512]{1,0:T(1,128)} %bitcast.9, ...), custom_call_target="tpu_custom_call" | custom-call | tf_op jit(solution)/shard_map/pallas_call | solution.py:391
  13.3 0.7 %copy.10 = f32[32,512]{1,0:T(8,128)} copy(f32[32,512]{1,0:T(8,128)S(1)} %shard_map.82) | data formatting | bytes 131072

commit v6 on v5

--- a/solution.py
+++ b/solution.py
@@ -294,7 +294,9 @@
                 wanted = jnp.floor((code + 0.5) * (1.0 / cols))
                 column = (code - cols * wanted).astype(jnp.int32)
                 pick = one_hot(iota((cols, LANES), 0) == column)
-                columns = dot(pieces, jnp.concatenate([pick, pick], axis=0))
+                pick = jnp.concatenate([pick, pick], axis=0)
+                half = (slots + 1) // 2 * levels
+                columns = jnp.concatenate([dot(pieces[:half], pick), dot(pieces[half:], pick)], axis=0)
                 answer = jnp.zeros((levels, LANES), F32)
                 for slot in range(slots):
                     weight = jnp.where(

time: 14.1 us -> 14.1 us (level)
  no operation moved by 1% of the time
where the time goes in v6:
time: 14.1 us; the launch traced here: 13.9 us
  Pallas kernels  12.6 us (89%)
  local copies, waits for them, and re-layouts  0.65 us (5%)
  between operations  0.65 us (5%)
    pallas_call x1, Pallas kernels, on_device(): pl.pallas_call(functools.partial(scoped, tiles, groups, near, cap, packs)...  12.6 us
    unnamed x1, local copies, waits for them, and re-layouts  0.65 us

profile of v6, /device:TPU:0, one launch (start us, length us, event | category | flops | bytes accessed | tf_op | source)
XLA Modules:
  0.0 13.9 jit_solution(16435609369554237229)
XLA Ops:
  0.7 12.6 %shard_map.82 = f32[32,512]{1,0:T(8,128)S(1)} custom-call(bf16[20,7,32,128]{3,2,1,0:T(8,128)(2,1)} %refs_0_.1, bf16[640,128]{1,0:T(8,128)(2,1)} %bitcast.5, bf16[32,32]{1,0:T(8,128)(2,1)} %refs_2_.1, s32[1,512]{1,0:T(1,128)} %bitcast.6, s32[1,512]{1,0:T(1,128)} %bitcast.7, s32[1,512]{1,0:T(1,128)} %bitcast.8, f32[1,512]{1,0:T(1,128)} %bitcast.9, ...), custom_call_target="tpu_custom_call" | custom-call | tf_op jit(solution)/shard_map/pallas_call | solution.py:393
  13.3 0.7 %copy.10 = f32[32,512]{1,0:T(8,128)} copy(f32[32,512]{1,0:T(8,128)S(1)} %shard_map.82) | data formatting | bytes 131072
